TPU v7x, 8 devices: a whole 2x2x1 slice. The times are simulated.
8 devices in a mesh: dp: 1 (over z), tp: 2 (over y), cp: 4 (over x, core).
Axes of the slice: x: 2, y: 2, z: 1, core: 2. Of those that a mesh axis runs over, the one named last changes fastest.
Arguments:
- x: bfloat16 [2048, 3072], P(('dp', 'cp'))
- doc_ids: int32 [2048], P(('dp', 'cp'))
- w_query: bfloat16 [3072, 3072], P(None, 'tp')
- w_key: bfloat16 [3072, 1024], P(None, 'tp')
- w_value: bfloat16 [3072, 1024], P(None, 'tp')
- w_out: bfloat16 [3072, 3072], P('tp')
Outputs:
- output: bfloat16 [2048, 3072], P(('dp', 'cp'))
All inputs are finite; a program needn't handle non-finite values.
Results may differ from a plain program's by a relative error of at most 0.00727143.
Values are sent between devices in bfloat16 or wider.
A program may use at most 1 GiB of HBM per device.

v0:
```python
import jax
import jax.numpy as jnp
from jax import lax
from jax.sharding import PartitionSpec as P

HEAD_DIM = 128


def block_update(soft_state, q_blk, k_blk, v_blk, allowed):
    run_max, run_sum, out_acc = soft_state
    scores = jnp.einsum('qhgd,khd->qhgk', q_blk, k_blk, preferred_element_type=jnp.float32) * (HEAD_DIM ** -0.5)
    scores = jnp.where(allowed[:, None, None, :], scores, -jnp.inf)
    new_max = jnp.maximum(run_max, jnp.max(scores, axis=-1))
    safe_max = jnp.where(new_max == -jnp.inf, 0.0, new_max)
    prob_vals = jnp.exp(scores - safe_max[..., None])
    rescale = jnp.exp(run_max - safe_max)
    run_sum = run_sum * rescale + jnp.sum(prob_vals, axis=-1)
    out_acc = out_acc * rescale[..., None] + jnp.einsum('qhgk,khd->qhgd', prob_vals.astype(jnp.bfloat16), v_blk, preferred_element_type=jnp.float32)
    return new_max, run_sum, out_acc


def solution(mesh):
    cp_size = mesh.shape['cp']
    shift_pairs = [(dev_idx, (dev_idx + 1) % cp_size) for dev_idx in range(cp_size)]

    def local_attention(x_loc, seg_loc, w_query, w_key, w_value, w_out):
        chunk_len = x_loc.shape[0]
        kv_heads = w_key.shape[1] // HEAD_DIM
        q_per_kv = w_query.shape[1] // w_key.shape[1]
        cp_rank = lax.axis_index('cp')
        q_loc = jnp.dot(x_loc, w_query, preferred_element_type=jnp.float32).astype(jnp.bfloat16).reshape(chunk_len, kv_heads, q_per_kv, HEAD_DIM)
        k_loc = jnp.dot(x_loc, w_key, preferred_element_type=jnp.float32).astype(jnp.bfloat16).reshape(chunk_len, kv_heads, HEAD_DIM)
        v_loc = jnp.dot(x_loc, w_value, preferred_element_type=jnp.float32).astype(jnp.bfloat16).reshape(chunk_len, kv_heads, HEAD_DIM)
        q_pos = cp_rank * chunk_len + jnp.arange(chunk_len)

        def visit_block(soft_state, k_blk, v_blk, seg_kv, src_chunk):
            k_pos = src_chunk * chunk_len + jnp.arange(chunk_len)
            active = (src_chunk <= cp_rank) & (seg_kv[chunk_len - 1] >= seg_loc[0])
            allowed = (seg_loc[:, None] == seg_kv[None, :]) & (q_pos[:, None] >= k_pos[None, :])
            return lax.cond(active, lambda same_state: block_update(same_state, q_loc, k_blk, v_blk, allowed), lambda same_state: same_state, soft_state)

        init_state = (jnp.full((chunk_len, kv_heads, q_per_kv), -jnp.inf, jnp.float32), jnp.zeros((chunk_len, kv_heads, q_per_kv), jnp.float32), jnp.zeros((chunk_len, kv_heads, q_per_kv, HEAD_DIM), jnp.float32))
        soft_state = visit_block(init_state, k_loc, v_loc, seg_loc, cp_rank)

        def shift_step(step_idx, loop_state):
            soft_state, k_blk, v_blk, seg_kv = loop_state
            k_blk = lax.ppermute(k_blk, 'cp', shift_pairs)
            v_blk = lax.ppermute(v_blk, 'cp', shift_pairs)
            seg_kv = lax.ppermute(seg_kv, 'cp', shift_pairs)
            src_chunk = (cp_rank - step_idx) % cp_size
            soft_state = visit_block(soft_state, k_blk, v_blk, seg_kv, src_chunk)
            return soft_state, k_blk, v_blk, seg_kv

        soft_state = lax.fori_loop(1, cp_size, shift_step, (soft_state, k_loc, v_loc, seg_loc))[0]
        heads_out = (soft_state[2] / soft_state[1][..., None]).astype(jnp.bfloat16).reshape(chunk_len, kv_heads * q_per_kv * HEAD_DIM)
        part_out = jnp.dot(heads_out, w_out, preferred_element_type=jnp.float32)
        return lax.psum(part_out, 'tp').astype(jnp.bfloat16)

    return jax.shard_map(local_attention, mesh=mesh, in_specs=(P(('dp', 'cp'), None), P(('dp', 'cp')), P(None, 'tp'), P(None, 'tp'), P(None, 'tp'), P('tp', None)), out_specs=P(('dp', 'cp'), None), check_vma=False)
```

profile of v0, /device:TPU:0, one launch (start us, length us, event | category | flops | bytes accessed | tf_op | source)
XLA Modules:
  0.0 263.5 jit_solution(11826972032445860997)
XLA Ops:
  0.0 1.5 fusion.35
  2.8 0.0 copy-start.10
  2.8 4.7 %convolution_convert_fusion.2 = bf16[512,512]{0,1:T(8,128)(2,1)} fusion(bf16[512,3072]{1,0:T(8,128)(2,1)S(1)} %copy-done, bf16[3072,512]{1,0:T(8,128)(2,1)} %param.15), kind=kOutput, calls=%fused_computation.48 | convolution fusion | flops 1610874880 | bytes 6815744 | tf_op jit(solution)/shard_map/dot_general | solution.py:32
  7.5 6.1 %convolution_convert_fusion = bf16[512,1536]{1,0:T(8,128)(2,1)} fusion(bf16[512,3072]{1,0:T(8,128)(2,1)S(1)} %copy-done, bf16[3072,1536]{1,0:T(8,128)(2,1)S(1)} %copy-done.10), kind=kOutput, calls=%fused_computation.46 | convolution fusion | flops 4832624640 | bytes 14155776 | tf_op jit(solution)/shard_map/dot_general | solution.py:31
  13.6 2.6 copy.17
  16.3 4.7 %convolution_convert_fusion.1 = bf16[512,512]{0,1:T(8,128)(2,1)} fusion(bf16[512,3072]{1,0:T(8,128)(2,1)S(1)} %copy-done, bf16[3072,512]{1,0:T(8,128)(2,1)} %param.16), kind=kOutput, calls=%fused_computation.47 | convolution fusion | flops 1610874880 | bytes 6815744 | tf_op jit(solution)/shard_map/dot_general | solution.py:33
  21.0 10.6 %conditional.2 = (f32[512,4,3]{0,2,1:T(4,128)S(1)}, f32[512,4,3]{0,2,1:T(4,128)S(1)}, f32[512,4,3,128]{3,0,2,1:T(8,128)}) conditional(s32[]{:T(128)} %bitcast.13, () %tuple.47, (s32[512]{0:T(512)S(1)}, s32[]{:T(128)}, s32[512,1]{0,1:T(1,128)S(1)}, s32[1,512]{1,0:T(1,128)S(1)}, bf16[512,4,128]{0,2,1:T(8,128)(2,1)S(1)}, ...), branch_computations={%region_0.0_spmd, %region_1.4_spmd} | conditional | flops 1646820352 | bytes 47143028 | solution.py:40
  21.2 0.3 compare_and_fusion
  21.5 2.2 fusion.4
  23.7 2.6 fusion.3
  26.4 5.2 %bitcast_add_fusion = f32[512,4,3,128]{3,0,2,1:T(8,128)} fusion(f32[4,512,512,3]{2,1,3,0:T(8,128)S(1)} %get-tuple-element.502, f32[512,4,3]{0,2,1:T(4,128)S(1)} %compare_select_fusion, pred[512,512]{0,1:T(8,128)(4,1)S(1)} %compare_and_fusion, f32[512,4,3]{0,2,1:T(4,128)S(1)} %get-tuple-element.499, bf16[512,4,128]{0,2,1:T(8,128)(2,1)S(1)} %copy-done.8), kind=kOutput, calls=%fused_computation.11 | convolution fusion | flops 818675712 | bytes 16564224 | tf_op jit(solution)/shard_map/cond/branch_1_fun/qhgk,khd->qhgd/dot_general | solution.py:18
  31.6 1.0 copy.21
  32.6 2.0 copy.22
  34.6 0.9 copy.23
  35.5 72.9 %while.26 = (s32[]{:T(128)}, f32[512,4,3]{0,2,1:T(4,128)S(1)}, f32[512,4,3]{0,2,1:T(4,128)S(1)}, f32[512,4,3,128]{3,0,2,1:T(8,128)}, bf16[512,4,128]{2,0,1:T(8,1...) while((s32[]{:T(128)}, f32[512,4,3]{0,2,1:T(4,128)S(1)}, ...), condition=%wide.region_9.10_spmd.clone, body=%wide.region_4.9_spmd.clone.sunk | while | flops 1647612928 | bytes 54452820 | solution.py:54
  35.5 0.9 collective-permute-start.1
  36.4 2.6 collective-permute-start.2
  39.0 0.0 collective-permute-start
  39.1 0.5 slice.35
  39.5 11.3 %collective-permute-done = s32[512]{0:T(512)S(1)} collective-permute-done((s32[512]{0:T(512)S(1)}, s32[512]{0:T(512)S(1)}, u32[]{:S(2)}, u32[]{:S(2)}) %collective-permute-start) | collective-permute-done | bytes 2080 | tf_op jit(solution)/shard_map/while/body/eval_jaxpr/ppermute | solution.py:49
  50.8 0.6 slice.34
  52.6 0.0 collective-permute-done.1
  52.6 0.0 collective-permute-done.2
  52.6 0.8 copy.66
  53.4 0.8 copy.67
  54.2 11.9 %collective-permute-start.1 = (bf16[512,4,128]{2,0,1:T(8,128)(2,1)}, bf16[512,4,128]{2,0,1:T(8,128)(2,1)S(1)}, u32[]{:S(2)}, u32[]{:S(2)}) collective-permute-start(bf16[512,4,128]{2,0,1:T(8,128)(2,1)} %get-tuple-element.611), channel_id=1, source_target_pairs={{0,1},{1,2},{2,3},{3,0},{4,5},{5,6},{6,7},{7,4}} | collective-permute-start | bytes 1572872 | tf_op jit(solution)/shard_map/while/body/eval_jaxpr/ppermute | solution.py:47
  66.1 2.5 collective-permute-start.2
  68.6 0.0 collective-permute-start
  68.6 0.5 slice.35
  69.1 8.8 %collective-permute-done = s32[512]{0:T(512)S(1)} collective-permute-done((s32[512]{0:T(512)S(1)}, s32[512]{0:T(512)S(1)}, u32[]{:S(2)}, u32[]{:S(2)}) %collective-permute-start) | collective-permute-done | bytes 2080 | tf_op jit(solution)/shard_map/while/body/eval_jaxpr/ppermute | solution.py:49
  77.9 0.6 slice.34
  79.6 0.0 collective-permute-done.1
  79.7 0.8 copy.66
  80.5 0.8 copy.67
  81.3 2.4 collective-permute-start.1
  83.7 2.5 collective-permute-start.2
  86.2 6.8 %collective-permute-start = (s32[512]{0:T(512)S(1)}, s32[512]{0:T(512)S(1)}, u32[]{:S(2)}, u32[]{:S(2)}) collective-permute-start(s32[512]{0:T(512)S(1)} %get-tuple-element.613), channel_id=1, source_target_pairs={{0,1},{1,2},{2,3},{3,0},{4,5},{5,6},{6,7},{7,4}} | collective-permute-start | bytes 6152 | tf_op jit(solution)/shard_map/while/body/eval_jaxpr/ppermute | solution.py:49
  93.0 0.5 slice.35
  93.5 11.5 %collective-permute-done = s32[512]{0:T(512)S(1)} collective-permute-done((s32[512]{0:T(512)S(1)}, s32[512]{0:T(512)S(1)}, u32[]{:S(2)}, u32[]{:S(2)}) %collective-permute-start) | collective-permute-done | bytes 2080 | tf_op jit(solution)/shard_map/while/body/eval_jaxpr/ppermute | solution.py:49
  105.0 0.6 slice.34
  106.7 0.0 collective-permute-done.2
  106.8 0.8 copy.66
  107.6 0.8 copy.67
  108.4 2.4 copy.24
  110.8 0.4 divide_convert_fusion
  111.2 0.0 copy-start.1
  111.2 10.9 %fusion.36 = f32[512,3072]{1,0:T(8,128)} fusion(bf16[512,1536]{0,1:T(8,128)(2,1)S(1)} %bitcast.75, bf16[1536,3072]{1,0:T(8,128)(2,1)} %param.17), kind=kOutput, calls=%fused_computation.50 | convolution fusion | flops 4831838208 | bytes 17301504 | tf_op jit(solution)/shard_map/dot_general | solution.py:56
  122.1 141.4 %all-reduce.1 = bf16[512,3072]{1,0:T(8,128)(2,1)} all-reduce(f32[512,3072]{1,0:T(8,128)} %fusion.36), channel_id=1, replica_groups=mesh['dp'=1,'tp'=2,'cp'=4] {'tp'}, use_global_device_ids=true, to_apply=%region_10.11 | all-reduce | flops 1572864 | bytes 9437184 | tf_op jit(solution)/shard_map/psum | solution.py:57
  (41 shorter events, 0.2 us)
Async XLA Ops:
  0.0 2.8 %copy-start = (bf16[512,3072]{1,0:T(8,128)(2,1)S(1)}, bf16[512,3072]{1,0:T(8,128)(2,1)}, u32[]{:S(2)}) copy-start(bf16[512,3072]{1,0:T(8,128)(2,1)} %param.12) | copy-start | bytes 9437188
  2.8 4.7 %copy-start.10 = (bf16[3072,1536]{1,0:T(8,128)(2,1)S(1)}, bf16[3072,1536]{1,0:T(8,128)(2,1)}, u32[]{:S(2)}) copy-start(bf16[3072,1536]{1,0:T(8,128)(2,1)} %param.14) | copy-start | bytes 28311556
  16.3 4.7 %copy-start.2 = (bf16[512,1536]{0,1:T(8,128)(2,1)S(1)}, bf16[512,1536]{0,1:T(8,128)(2,1)}, u32[]{:S(2)}) copy-start(bf16[512,1536]{0,1:T(8,128)(2,1)} %copy.17) | copy-start | bytes 4718596
  16.3 4.7 %copy-start.6 = (bf16[512,512]{0,1:T(8,128)(2,1)S(1)}, bf16[512,512]{0,1:T(8,128)(2,1)}, u32[]{:S(2)}) copy-start(bf16[512,512]{0,1:T(8,128)(2,1)} %convolution_convert_fusion.2) | copy-start | bytes 1572868
  16.3 4.7 %copy-start.9 = (s32[512]{0:T(512)S(1)}, s32[512]{0:T(512)}, u32[]{:S(2)}) copy-start(s32[512]{0:T(512)} %param.13) | copy-start | bytes 6148
  21.0 10.6 %copy-start.7 = (bf16[512,512]{0,1:T(8,128)(2,1)S(1)}, bf16[512,512]{0,1:T(8,128)(2,1)}, u32[]{:S(2)}) copy-start(bf16[512,512]{0,1:T(8,128)(2,1)} %convolution_convert_fusion.2) | copy-start | bytes 1572868
  23.7 2.6 copy-start.4
  23.7 2.6 %copy-start.8 = (bf16[512,4,128]{0,2,1:T(8,128)(2,1)S(1)}, bf16[512,4,128]{0,2,1:T(8,128)(2,1)}, u32[]{:S(2)}) copy-start(bf16[512,4,128]{0,2,1:T(8,128)(2,1)} %get-tuple-element.458) | copy-start | bytes 1572868 | tf_op jit(solution)/shard_map/cond
  26.4 5.2 %copy-start.5 = (f32[512,4,3]{0,2,1:T(4,128)S(1)}, f32[512,4,3]{0,2,1:T(4,128)}, u32[]{:S(2)}) copy-start(f32[512,4,3]{0,2,1:T(4,128)} %copy-done.4) | copy-start | bytes 73732 | tf_op jit(solution)/shard_map/cond
  31.6 3.1 %copy-start.3 = (bf16[512,1536]{0,1:T(8,128)(2,1)S(1)}, bf16[512,1536]{0,1:T(8,128)(2,1)}, u32[]{:S(2)}) copy-start(bf16[512,1536]{0,1:T(8,128)(2,1)} %copy.17) | copy-start | bytes 4718596
  35.5 17.0 %collective-permute-start.1 = (bf16[512,4,128]{2,0,1:T(8,128)(2,1)}, bf16[512,4,128]{2,0,1:T(8,128)(2,1)S(1)}, u32[]{:S(2)}, u32[]{:S(2)}) collective-permute-start(bf16[512,4,128]{2,0,1:T(8,128)(2,1)} %get-tuple-element.611), channel_id=1, source_target_pairs={{0,1},{1,2},{2,3},{3,0},{4,5},{5,6},{6,7},{7,4}} | collective-permute-start | bytes 1572872 | tf_op jit(solution)/shard_map/while/body/eval_jaxpr/ppermute | solution.py:47
  36.4 16.1 %collective-permute-start.2 = (bf16[512,4,128]{2,0,1:T(8,128)(2,1)}, bf16[512,4,128]{2,0,1:T(8,128)(2,1)S(1)}, u32[]{:S(2)}, u32[]{:S(2)}) collective-permute-start(bf16[512,4,128]{2,0,1:T(8,128)(2,1)} %get-tuple-element.612), channel_id=1, source_target_pairs={{0,1},{1,2},{2,3},{3,0},{4,5},{5,6},{6,7},{7,4}} | collective-permute-start | bytes 1572872 | tf_op jit(solution)/shard_map/while/body/eval_jaxpr/ppermute | solution.py:48
  39.0 11.8 %collective-permute-start = (s32[512]{0:T(512)S(1)}, s32[512]{0:T(512)S(1)}, u32[]{:S(2)}, u32[]{:S(2)}) collective-permute-start(s32[512]{0:T(512)S(1)} %get-tuple-element.613), channel_id=1, source_target_pairs={{0,1},{1,2},{2,3},{3,0},{4,5},{5,6},{6,7},{7,4}} | collective-permute-start | bytes 6152 | tf_op jit(solution)/shard_map/while/body/eval_jaxpr/ppermute | solution.py:49
  54.2 25.4 %collective-permute-start.1 = (bf16[512,4,128]{2,0,1:T(8,128)(2,1)}, bf16[512,4,128]{2,0,1:T(8,128)(2,1)S(1)}, u32[]{:S(2)}, u32[]{:S(2)}) collective-permute-start(bf16[512,4,128]{2,0,1:T(8,128)(2,1)} %get-tuple-element.611), channel_id=1, source_target_pairs={{0,1},{1,2},{2,3},{3,0},{4,5},{5,6},{6,7},{7,4}} | collective-permute-start | bytes 1572872 | tf_op jit(solution)/shard_map/while/body/eval_jaxpr/ppermute | solution.py:47
  66.1 13.6 %collective-permute-start.2 = (bf16[512,4,128]{2,0,1:T(8,128)(2,1)}, bf16[512,4,128]{2,0,1:T(8,128)(2,1)S(1)}, u32[]{:S(2)}, u32[]{:S(2)}) collective-permute-start(bf16[512,4,128]{2,0,1:T(8,128)(2,1)} %get-tuple-element.612), channel_id=1, source_target_pairs={{0,1},{1,2},{2,3},{3,0},{4,5},{5,6},{6,7},{7,4}} | collective-permute-start | bytes 1572872 | tf_op jit(solution)/shard_map/while/body/eval_jaxpr/ppermute | solution.py:48
  68.6 9.3 %collective-permute-start = (s32[512]{0:T(512)S(1)}, s32[512]{0:T(512)S(1)}, u32[]{:S(2)}, u32[]{:S(2)}) collective-permute-start(s32[512]{0:T(512)S(1)} %get-tuple-element.613), channel_id=1, source_target_pairs={{0,1},{1,2},{2,3},{3,0},{4,5},{5,6},{6,7},{7,4}} | collective-permute-start | bytes 6152 | tf_op jit(solution)/shard_map/while/body/eval_jaxpr/ppermute | solution.py:49
  81.3 25.4 %collective-permute-start.1 = (bf16[512,4,128]{2,0,1:T(8,128)(2,1)}, bf16[512,4,128]{2,0,1:T(8,128)(2,1)S(1)}, u32[]{:S(2)}, u32[]{:S(2)}) collective-permute-start(bf16[512,4,128]{2,0,1:T(8,128)(2,1)} %get-tuple-element.611), channel_id=1, source_target_pairs={{0,1},{1,2},{2,3},{3,0},{4,5},{5,6},{6,7},{7,4}} | collective-permute-start | bytes 1572872 | tf_op jit(solution)/shard_map/while/body/eval_jaxpr/ppermute | solution.py:47
  83.7 23.0 %collective-permute-start.2 = (bf16[512,4,128]{2,0,1:T(8,128)(2,1)}, bf16[512,4,128]{2,0,1:T(8,128)(2,1)S(1)}, u32[]{:S(2)}, u32[]{:S(2)}) collective-permute-start(bf16[512,4,128]{2,0,1:T(8,128)(2,1)} %get-tuple-element.612), channel_id=1, source_target_pairs={{0,1},{1,2},{2,3},{3,0},{4,5},{5,6},{6,7},{7,4}} | collective-permute-start | bytes 1572872 | tf_op jit(solution)/shard_map/while/body/eval_jaxpr/ppermute | solution.py:48
  86.2 18.8 %collective-permute-start = (s32[512]{0:T(512)S(1)}, s32[512]{0:T(512)S(1)}, u32[]{:S(2)}, u32[]{:S(2)}) collective-permute-start(s32[512]{0:T(512)S(1)} %get-tuple-element.613), channel_id=1, source_target_pairs={{0,1},{1,2},{2,3},{3,0},{4,5},{5,6},{6,7},{7,4}} | collective-permute-start | bytes 6152 | tf_op jit(solution)/shard_map/while/body/eval_jaxpr/ppermute | solution.py:49
  111.2 152.3 %copy-start.1 = (bf16[512,3072]{1,0:T(8,128)(2,1)S(1)}, bf16[512,3072]{1,0:T(8,128)(2,1)}, u32[]{:S(2)}) copy-start(bf16[512,3072]{1,0:T(8,128)(2,1)} %param.12) | copy-start | bytes 9437188
where the time goes:
time: 265 us; the launch traced here: 263 us
  blocking collectives  141 us (53%)
  matrix products  33.8 us (13%)
  waiting for transfers between devices  31.7 us (12%)
  starting transfers between devices  29.7 us (11%)
  local copies, waits for them, and re-layouts  18.4 us (7%)
  loops' own time  3.86 us (1%)
  other arithmetic  3.36 us (1%)
    psum x1, blocking collectives, local_attention(): return lax.psum(part_out, 'tp').astype(jnp.bfloat16)  141 us
    ppermute x3, waiting for transfers between devices, shift_step(): seg_kv = lax.ppermute(seg_kv, 'cp', shift_pairs)  31.7 us
    ppermute x3, starting transfers between devices, shift_step(): k_blk = lax.ppermute(k_blk, 'cp', shift_pairs)  15.2 us
    dot_general x1, matrix products, local_attention(): part_out = jnp.dot(heads_out, w_out, preferred_element_type=jnp.float32)  10.9 us
    ppermute x3, starting transfers between devices, shift_step(): v_blk = lax.ppermute(v_blk, 'cp', shift_pairs)  7.6 us
    ppermute x3, starting transfers between devices, shift_step(): seg_kv = lax.ppermute(seg_kv, 'cp', shift_pairs)  6.87 us
    dot_general x1, matrix products, local_attention(): jnp.dot(x_loc, w_query, preferred_element_type=jnp.float32)  6.14 us
  transfers between devices with their start and end apart: 9, of which 3 were waited for; matrix products, arithmetic and copies ran while one was open for 1% of the time, Pallas kernels for 0%

commit v1 on v0

v1 whole, which is shorter than its diff:
```python
import math

import jax
import jax.numpy as jnp
from jax import lax
from jax.experimental import pallas as pl
from jax.experimental.pallas import tpu as pltpu
from jax.sharding import PartitionSpec as P

HEAD = 128
TILE = 256
COLS = 512
MESH = pl.DeviceIdType.MESH
F32 = jnp.float32
BF16 = jnp.bfloat16
SCALE = HEAD ** -0.5 * math.log2(math.e)


def layer_kernel(seg_hbm, x_hbm, wq_hbm, wk_hbm, wv_hbm, wo_hbm, y_hbm,
                 seg, segq, xbuf, wbuf, kv, q, o_own, o_oth, wo, w_oth, y_own, y_oth,
                 load_sem, tile_sem, out_sem, seg_s, seg_r, kv_s, kv_r,
                 y_s, y_r, xf_s, xf_r, d1_s, d1_r, d2_s, d2_r, o_s, o_r):
    chunk, width = xbuf.shape
    kv_heads = kv.shape[0] // 2
    heads = q.shape[0]
    group = heads // kv_heads
    n_blocks = seg.shape[0]
    quarter = wo.shape[0] // n_blocks
    pieces = y_s.shape[0]
    piece = quarter // pieces
    n_cols = width // COLS
    kv_tiles = 2 * kv_heads * HEAD // TILE
    q_tiles = heads * HEAD // TILE
    slots = wbuf.shape[0]

    dp = lax.axis_index('dp')
    tp = lax.axis_index('tp')
    me = lax.axis_index('cp')
    core_peer = me + 1 - 2 * lax.rem(me, 2)
    chip_peer = lax.rem(me + 2, 4)
    far_peer = 3 - me
    tp_peer = (dp, 1 - tp, me)

    def at(block):
        return (dp, tp, block)

    def remote(src, dst, s_sem, r_sem, where):
        return pltpu.make_async_remote_copy(src_ref=src, dst_ref=dst, send_sem=s_sem, recv_sem=r_sem,
                                            device_id=where, device_id_type=MESH)

    def kv_tile_src(t):
        per = kv_tiles // 2
        return (wk_hbm if t < per else wv_hbm).at[:, pl.ds((t % per) * TILE, TILE)]

    def tile_copy(src, slot):
        return pltpu.make_async_copy(src, wbuf.at[slot], tile_sem.at[slot])

    def q_tile_src(t):
        return wq_hbm.at[:, pl.ds(pl.multiple_of(t * TILE, TILE), TILE)]

    x_load = pltpu.make_async_copy(x_hbm, xbuf, load_sem.at[0])
    wo_load = pltpu.make_async_copy(wo_hbm, wo, load_sem.at[1])
    seg_load = pltpu.make_async_copy(seg_hbm, seg.at[me], load_sem.at[2])
    x_load.start()
    for t in range(kv_tiles):
        tile_copy(kv_tile_src(t), t).start()
    seg_load.start()

    barrier = pltpu.get_barrier_semaphore()
    for where in (tp_peer, at(core_peer), at(chip_peer), at(far_peer)):
        pl.semaphore_signal(barrier, inc=1, device_id=where, device_id_type=MESH)
    pl.semaphore_wait(barrier, 4)

    def rows_of(block, i):
        return pl.ds(pl.multiple_of(block * quarter + i * piece, piece), piece)

    def y_copy(i):
        return remote(wo_hbm.at[rows_of(me, i)], w_oth.at[rows_of(me, i)], y_s.at[i], y_r.at[i], tp_peer)

    def hand_on(block, i, s_sem, r_sem, where):
        part = w_oth.at[rows_of(block, i)]
        return remote(part, part, s_sem.at[i], r_sem.at[i], where)

    def seg_copy(k, block, where):
        return remote(seg.at[block], seg.at[block], seg_s.at[k], seg_r.at[k], where)

    def kv_copy(k, block, where):
        part = kv.at[:, pl.ds(pl.multiple_of(block * chunk, chunk), chunk), :]
        return remote(part, part, kv_s.at[k], kv_r.at[k], where)

    def o_copy(u):
        h = head_of(u)
        return remote(o_own.at[h], o_oth.at[h], o_s.at[u], o_r.at[u], tp_peer)

    def group_of(j):
        high = lax.rem(me // 2 + j // 2, 2)
        low = lax.rem(lax.rem(me, 2) + lax.rem(j, 2), 2)
        return 2 * high + low

    def head_of(u):
        return group_of(u // group) * group + lax.rem(u, group)

    for i in range(pieces):
        y_copy(i).start()
    seg_load.wait()
    for k, block in enumerate((core_peer, chip_peer, far_peer)):
        seg_copy(k, me, at(block)).start()

    x_load.wait()
    own_rows = pl.ds(pl.multiple_of(me * chunk, chunk), chunk)

    def project_kv(t, _):
        tile_copy(wk_hbm.at[:, pl.ds(0, TILE)], t).wait()
        part = jnp.dot(xbuf[...], wbuf[t], preferred_element_type=F32).astype(BF16)
        for k in range(TILE // HEAD):
            kv[t * (TILE // HEAD) + k, own_rows, :] = part[:, k * HEAD:(k + 1) * HEAD]

        @pl.when(t < q_tiles)
        def _():
            tile_copy(q_tile_src(t), t).start()
        return 0

    lax.fori_loop(0, kv_tiles, project_kv, 0)

    def project_q(t, _):
        slot = lax.rem(t, slots)
        tile_copy(q_tile_src(t), slot).wait()
        part = jnp.dot(xbuf[...], wbuf[slot], preferred_element_type=F32).astype(BF16)
        for k in range(TILE // HEAD):
            q[t * (TILE // HEAD) + k] = part[:, k * HEAD:(k + 1) * HEAD]

        @pl.when(t + slots < q_tiles)
        def _():
            tile_copy(q_tile_src(t + slots), slot).start()

        @pl.when(t == 0)
        def _():
            @pl.when(me < 2)
            def _():
                kv_copy(0, me, at(chip_peer)).start()
            kv_copy(1, me, at(core_peer)).start()
            wo_load.start()
        return 0

    lax.fori_loop(0, q_tiles, project_q, 0)

    def pass_y(i):
        y_copy(i).wait_recv()
        hand_on(me, i, xf_s, xf_r, at(chip_peer)).start()
        hand_on(me, i, d1_s, d1_r, at(core_peer)).start()

    def pass_x(i):
        hand_on(chip_peer, i, xf_s, xf_r, at(chip_peer)).wait_recv()
        hand_on(chip_peer, i, d2_s, d2_r, at(core_peer)).start()

    pass_y(0)
    for k, block in enumerate((core_peer, chip_peer, far_peer)):
        seg_copy(k, block, at(block)).wait_recv()
    seg_col = jnp.transpose(jnp.broadcast_to(seg[me], (HEAD, chunk)))
    segq[...] = seg_col

    kv_copy(1, core_peer, at(core_peer)).wait_recv()

    @pl.when(me >= 2)
    def _():
        kv_copy(0, chip_peer, at(chip_peer)).wait_recv()
        kv_copy(2, chip_peer, at(core_peer)).start()
        kv_copy(2, far_peer, at(core_peer)).wait_recv()

    def attend(h, g, r, n):
        rows = pl.ds(pl.multiple_of(r * TILE, TILE), TILE)
        q_t = q[h, rows, :]
        sq = segq[rows, :]
        sq = jnp.concatenate([sq] * (chunk // HEAD), axis=1)
        parts = []
        for b in range(n):
            s = lax.dot_general(q_t, kv[g, pl.ds(b * chunk, chunk), :], (((1,), (1,)), ((), ())), preferred_element_type=F32)
            ok = sq == seg[b]
            if b == n - 1:
                q_pos = r * TILE + lax.broadcasted_iota(jnp.int32, (TILE, chunk), 0)
                ok = ok & (q_pos >= lax.broadcasted_iota(jnp.int32, (TILE, chunk), 1))
            parts.append(jnp.where(ok, s, -jnp.inf))
        top = parts[0].max(axis=1, keepdims=True)
        for s in parts[1:]:
            top = jnp.maximum(top, s.max(axis=1, keepdims=True))
        total = None
        acc = None
        for b, s in enumerate(parts):
            p = jnp.exp2((s - top) * SCALE)
            row_sum = p.sum(axis=1, keepdims=True)
            pv = jnp.dot(p.astype(BF16), kv[kv_heads + g, pl.ds(b * chunk, chunk), :], preferred_element_type=F32)
            total = row_sum if total is None else total + row_sum
            acc = pv if acc is None else acc + pv
        o_own[h, rows, :] = (acc / total).astype(BF16)

    def attend_head(u, _):
        g = group_of(u // group)
        h = head_of(u)
        for n in range(1, n_blocks + 1):
            @pl.when(me == n - 1)
            def _(n=n):
                def one(r, c):
                    attend(h, g, r, n)
                    return c
                lax.fori_loop(0, chunk // TILE, one, 0)

        @pl.when(u > 0)
        def _():
            o_copy(u - 1).start()

        @pl.when(u == group - 1)
        def _():
            pass_y(1)

        @pl.when(u == 3 * group - 1)
        def _():
            pass_x(0)
        return 0

    lax.fori_loop(0, heads, attend_head, 0)
    pass_y(2)

    def add_rows(o_ref, w_ref, y_ref, h0, count, first):
        rows = pl.ds(pl.multiple_of(h0 * HEAD, HEAD), count * HEAD)

        def one(c, carry):
            cols = pl.ds(pl.multiple_of(c * COLS, COLS), COLS)
            left = jnp.concatenate([o_ref[h0 + k] for k in range(count)], axis=1)
            part = jnp.dot(left, w_ref[rows, cols], preferred_element_type=F32)
            y_ref[:, cols] = part if first else y_ref[:, cols] + part
            return carry

        lax.fori_loop(0, n_cols, one, 0)

    wo_load.wait()
    add_rows(o_own, wo, y_own, group_of(0) * group, group, True)
    o_copy(heads - 1).start()
    for j in range(1, kv_heads - 1):
        add_rows(o_own, wo, y_own, group_of(j) * group, group, False)
    last = group_of(kv_heads - 1) * group
    add_rows(o_own, wo, y_own, last, group - 1, False)
    add_rows(o_own, wo, y_own, last + group - 1, 1, False)

    pass_x(1)
    for u in range(group):
        o_copy(u).wait_recv()
    add_rows(o_oth, w_oth, y_oth, group_of(0) * group, group, True)
    for i in range(pieces):
        hand_on(core_peer, i, d1_s, d1_r, at(core_peer)).wait_recv()
    for u in range(group, 2 * group):
        o_copy(u).wait_recv()
    add_rows(o_oth, w_oth, y_oth, group_of(1) * group, group, False)
    pass_x(2)
    for u in range(2 * group, 3 * group):
        o_copy(u).wait_recv()
    add_rows(o_oth, w_oth, y_oth, group_of(2) * group, group, False)
    for i in range(pieces):
        hand_on(far_peer, i, d2_s, d2_r, at(core_peer)).wait_recv()
    for u in range(3 * group, heads - 1):
        o_copy(u).wait_recv()
    add_rows(o_oth, w_oth, y_oth, last, group - 1, False)
    o_copy(heads - 1).wait_recv()

    def out_copy(c):
        cols = pl.ds(pl.multiple_of(c * COLS, COLS), COLS)
        return pltpu.make_async_copy(xbuf.at[:, cols], y_hbm.at[:, cols], out_sem.at[c])

    def finish(c, carry):
        h = last + group - 1
        cols = pl.ds(pl.multiple_of(c * COLS, COLS), COLS)
        part = jnp.dot(o_oth[h], w_oth[pl.ds(pl.multiple_of(h * HEAD, HEAD), HEAD), cols], preferred_element_type=F32)
        xbuf[:, cols] = (y_own[:, cols] + (y_oth[:, cols] + part)).astype(BF16)
        out_copy(c).start()
        return carry

    lax.fori_loop(0, n_cols, finish, 0)

    for i in range(pieces):
        y_copy(i).wait_send()
        hand_on(me, i, xf_s, xf_r, at(chip_peer)).wait_send()
        hand_on(me, i, d1_s, d1_r, at(core_peer)).wait_send()
        hand_on(chip_peer, i, d2_s, d2_r, at(core_peer)).wait_send()
    for k, block in enumerate((core_peer, chip_peer, far_peer)):
        seg_copy(k, me, at(block)).wait_send()
    kv_copy(1, me, at(core_peer)).wait_send()

    @pl.when(me < 2)
    def _():
        kv_copy(0, me, at(chip_peer)).wait_send()

    @pl.when(me >= 2)
    def _():
        kv_copy(2, chip_peer, at(core_peer)).wait_send()

    for u in range(heads):
        o_copy(u).wait_send()
    for c in range(n_cols):
        out_copy(c).wait()


def solution(mesh):
    n_blocks = mesh.shape['cp']

    def layer(x_loc, seg_loc, w_query, w_key, w_value, w_out):
        chunk, width = x_loc.shape
        kv_heads = w_key.shape[1] // HEAD
        heads = w_query.shape[1] // HEAD
        pieces = 3
        dma = pltpu.SemaphoreType.DMA
        any_spec = pl.BlockSpec(memory_space=pl.ANY)
        return pl.pallas_call(
            layer_kernel,
            out_shape=jax.ShapeDtypeStruct((chunk, width), BF16),
            in_specs=[any_spec] * 6,
            out_specs=any_spec,
            scratch_shapes=[
                pltpu.VMEM((n_blocks, 1, chunk), jnp.int32),
                pltpu.VMEM((chunk, HEAD), jnp.int32),
                pltpu.VMEM((chunk, width), BF16),
                pltpu.VMEM((4, width, TILE), BF16),
                pltpu.VMEM((2 * kv_heads, n_blocks * chunk, HEAD), BF16),
                pltpu.VMEM((heads, chunk, HEAD), BF16),
                pltpu.VMEM((heads, chunk, HEAD), BF16),
                pltpu.VMEM((heads, chunk, HEAD), BF16),
                pltpu.VMEM(w_out.shape, BF16),
                pltpu.VMEM(w_out.shape, BF16),
                pltpu.VMEM((chunk, width), F32),
                pltpu.VMEM((chunk, width), F32),
                dma((3,)), dma((4,)), dma((width // COLS,)),
                dma((3,)), dma((3,)), dma((3,)), dma((3,)),
                dma((pieces,)), dma((pieces,)), dma((pieces,)), dma((pieces,)),
                dma((pieces,)), dma((pieces,)), dma((pieces,)), dma((pieces,)),
                dma((heads,)), dma((heads,)),
            ],
            compiler_params=pltpu.CompilerParams(collective_id=0, has_side_effects=True, vmem_limit_bytes=67043328),
        )(seg_loc.reshape(1, chunk), x_loc, w_query, w_key, w_value, w_out)

    rows = P(('dp', 'cp'), None)
    return jax.shard_map(layer, mesh=mesh,
                         in_specs=(rows, P(('dp', 'cp')), P(None, 'tp'), P(None, 'tp'), P(None, 'tp'), P('tp', None)),
                         out_specs=rows, check_vma=False)
```

time: 265 us -> 97.2 us (0.37)
  blocking collectives: 141 us -> 0 us
  Pallas kernels: 0 us -> 93.3 us
  matrix products: 33.8 us -> 0 us
  waiting for transfers between devices: 31.7 us -> 0 us
  starting transfers between devices: 29.7 us -> 0 us
  local copies, waits for them, and re-layouts: 18.4 us -> 3.76 us
  loops' own time: 3.86 us -> 0 us
  other arithmetic: 3.36 us -> 0 us
    psum x1 -> x0, blocking collectives: 141 us -> none  [local_attention(): return lax.psum(part_out, 'tp').astype(jnp.bfloat16)]
    pallas_call x0 -> x1, Pallas kernels: none -> 93.3 us  [layer(): pl.pallas_call(layer_kernel, out_shape=jax.ShapeDtypeStruct((chunk, width...]
    dot_general x6 -> x0, matrix products: 33.8 us -> none  [the longest x1 10.9 us: local_attention(): part_out = jnp.dot(heads_out, w_out, preferred_element_type=jnp.float32)]
    ppermute x9 -> x0, waiting for transfers between devices: 31.7 us -> none  [the longest x3 31.7 us: shift_step(): seg_kv = lax.ppermute(seg_kv, 'cp', shift_pairs)]
    ppermute x9 -> x0, starting transfers between devices: 29.7 us -> none  [the longest x3 15.2 us: shift_step(): k_blk = lax.ppermute(k_blk, 'cp', shift_pairs)]
    while x10 -> x0, local copies, waits for them, and re-layouts: 7.15 us -> none
    slice x7 -> x0, local copies, waits for them, and re-layouts: 4.65 us -> none  [visit_block(): active = (src_chunk <= cp_rank) & (seg_kv[chunk_len - 1] >= seg_loc[0])]
    another operation x5 -> x0, loops' own time: 3.86 us -> none  [the longest x1 3.53 us: local_attention(): lax.fori_loop(1, cp_size, shift_step, (soft_state, k_loc, v_loc, seg_loc))]
  transfers between devices with their start and end apart: 9 -> 0, of which waited for: 3 -> 0; matrix products, arithmetic and copies ran while one was open for 1% -> 0% of each run, Pallas kernels for 0% -> 0%
where the time goes in v1:
time: 97.2 us; the launch traced here: 97.1 us
  Pallas kernels  93.3 us (96%)
  local copies, waits for them, and re-layouts  3.76 us (4%)
    pallas_call x1, Pallas kernels, layer(): pl.pallas_call(layer_kernel, out_shape=jax.ShapeDtypeStruct((chunk, width...  93.3 us
    unnamed x1, local copies, waits for them, and re-layouts  3.76 us

profile of v1, /device:TPU:0, one launch (start us, length us, event | category | flops | bytes accessed | tf_op | source)
XLA Modules:
  0.0 97.1 jit_solution(7684489397760965204)
XLA Ops:
  0.0 93.3 %shard_map.64 = bf16[512,3072]{1,0:T(8,128)(2,1)} custom-call(s32[1,512]{1,0:T(1,128)} %bitcast.1, bf16[512,3072]{1,0:T(8,128)(2,1)} %x_hbm.1, bf16[3072,1536]{1,0:T(8,128)(2,1)} %wq_hbm.1, bf16[3072,512]{1,0:T(8,128)(2,1)} %wk_hbm.1, bf16[3072,512]{1,0:T(8,128)(2,1)} %wv_hbm.1, bf16[1536,3072]{1,0:T(8,128)(2,1)} %wo_hbm.1), custom_call_target="tpu_custom_call" | custom-call | tf_op jit(solution)/shard_map/pallas_call | solution.py:311
  93.3 3.8 %copy.8 = bf16[512,3072]{1,0:T(8,128)(2,1)} copy(bf16[512,3072]{1,0:T(8,128)(2,1)} %shard_map.64) | data formatting | bytes 6291456

commit v2 on v1

--- a/solution.py
+++ b/solution.py
@@ -16,9 +16,9 @@
 SCALE = HEAD ** -0.5 * math.log2(math.e)
 
 
-def layer_kernel(seg_hbm, x_hbm, wq_hbm, wk_hbm, wv_hbm, wo_hbm, y_hbm,
+def layer_kernel(seg_hbm, x_hbm, wq_hbm, wk_hbm, wv_hbm, wo_hbm, y_out,
                  seg, segq, xbuf, wbuf, kv, q, o_own, o_oth, wo, w_oth, y_own, y_oth,
-                 load_sem, tile_sem, out_sem, seg_s, seg_r, kv_s, kv_r,
+                 load_sem, tile_sem, seg_s, seg_r, kv_s, kv_r,
                  y_s, y_r, xf_s, xf_r, d1_s, d1_r, d2_s, d2_r, o_s, o_r):
     chunk, width = xbuf.shape
     kv_heads = kv.shape[0] // 2
@@ -32,6 +32,7 @@
     kv_tiles = 2 * kv_heads * HEAD // TILE
     q_tiles = heads * HEAD // TILE
     slots = wbuf.shape[0]
+    ends = chunk // HEAD
 
     dp = lax.axis_index('dp')
     tp = lax.axis_index('tp')
@@ -59,8 +60,20 @@
         return wq_hbm.at[:, pl.ds(pl.multiple_of(t * TILE, TILE), TILE)]
 
     x_load = pltpu.make_async_copy(x_hbm, xbuf, load_sem.at[0])
-    wo_load = pltpu.make_async_copy(wo_hbm, wo, load_sem.at[1])
-    seg_load = pltpu.make_async_copy(seg_hbm, seg.at[me], load_sem.at[2])
+    seg_load = pltpu.make_async_copy(seg_hbm, seg.at[me], load_sem.at[1])
+
+    def rows_of(block, i):
+        return pl.ds(pl.multiple_of(block * quarter + i * piece, piece), piece)
+
+    def wo_piece_load(i):
+        return pltpu.make_async_copy(wo_hbm.at[rows_of(me, i)], wo.at[rows_of(me, i)], load_sem.at[2 + i])
+
+    def wo_rest_load(k, block):
+        rows = pl.ds(pl.multiple_of(block * quarter, quarter), quarter)
+        return pltpu.make_async_copy(wo_hbm.at[rows], wo.at[rows], load_sem.at[2 + pieces + k])
+
+    others = (core_peer, chip_peer, far_peer)
+    wo_piece_load(0).start()
     x_load.start()
     for t in range(kv_tiles):
         tile_copy(kv_tile_src(t), t).start()
@@ -71,11 +84,8 @@
         pl.semaphore_signal(barrier, inc=1, device_id=where, device_id_type=MESH)
     pl.semaphore_wait(barrier, 4)
 
-    def rows_of(block, i):
-        return pl.ds(pl.multiple_of(block * quarter + i * piece, piece), piece)
-
     def y_copy(i):
-        return remote(wo_hbm.at[rows_of(me, i)], w_oth.at[rows_of(me, i)], y_s.at[i], y_r.at[i], tp_peer)
+        return remote((wo if i == 0 else wo_hbm).at[rows_of(me, i)], w_oth.at[rows_of(me, i)], y_s.at[i], y_r.at[i], tp_peer)
 
     def hand_on(block, i, s_sem, r_sem, where):
         part = w_oth.at[rows_of(block, i)]
@@ -91,19 +101,34 @@
     def o_copy(u):
         h = head_of(u)
         return remote(o_own.at[h], o_oth.at[h], o_s.at[u], o_r.at[u], tp_peer)
+
+    def end_copy(r):
+        h = head_of(heads - 1)
+        rows = pl.ds(r * HEAD, HEAD)
+        return remote(o_own.at[h, rows], o_oth.at[h, rows], o_s.at[heads - 1 + r], o_r.at[heads - 1 + r], tp_peer)
 
     def group_of(j):
         high = lax.rem(me // 2 + j // 2, 2)
         low = lax.rem(lax.rem(me, 2) + lax.rem(j, 2), 2)
         return 2 * high + low
 
+    def place_of(u):
+        half = u // 6
+        v = u - 6 * half
+        end = v // 4
+        j = (1 - half) * (v // 3) + half * (2 + (1 - end) * (v // 2) + end * (v - 4))
+        i = (1 - half) * (v % 3) + half * ((1 - end) * (v % 2) + 2 * end)
+        return j, i
+
     def head_of(u):
-        return group_of(u // group) * group + lax.rem(u, group)
-
+        j, i = place_of(u)
+        return group_of(j) * group + i
+
+    wo_piece_load(0).wait()
     for i in range(pieces):
         y_copy(i).start()
     seg_load.wait()
-    for k, block in enumerate((core_peer, chip_peer, far_peer)):
+    for k, block in enumerate(others):
         seg_copy(k, me, at(block)).start()
 
     x_load.wait()
@@ -139,7 +164,10 @@
             def _():
                 kv_copy(0, me, at(chip_peer)).start()
             kv_copy(1, me, at(core_peer)).start()
-            wo_load.start()
+            for i in range(1, pieces):
+                wo_piece_load(i).start()
+            for k, block in enumerate(others):
+                wo_rest_load(k, block).start()
         return 0
 
     lax.fori_loop(0, q_tiles, project_q, 0)
@@ -154,7 +182,7 @@
         hand_on(chip_peer, i, d2_s, d2_r, at(core_peer)).start()
 
     pass_y(0)
-    for k, block in enumerate((core_peer, chip_peer, far_peer)):
+    for k, block in enumerate(others):
         seg_copy(k, block, at(block)).wait_recv()
     seg_col = jnp.transpose(jnp.broadcast_to(seg[me], (HEAD, chunk)))
     segq[...] = seg_col
@@ -194,8 +222,8 @@
         o_own[h, rows, :] = (acc / total).astype(BF16)
 
     def attend_head(u, _):
-        g = group_of(u // group)
         h = head_of(u)
+        g = h // group
         for n in range(1, n_blocks + 1):
             @pl.when(me == n - 1)
             def _(n=n):
@@ -232,55 +260,50 @@
 
         lax.fori_loop(0, n_cols, one, 0)
 
-    wo_load.wait()
-    add_rows(o_own, wo, y_own, group_of(0) * group, group, True)
-    o_copy(heads - 1).start()
-    for j in range(1, kv_heads - 1):
-        add_rows(o_own, wo, y_own, group_of(j) * group, group, False)
-    last = group_of(kv_heads - 1) * group
-    add_rows(o_own, wo, y_own, last, group - 1, False)
-    add_rows(o_own, wo, y_own, last + group - 1, 1, False)
+    for i in range(1, pieces):
+        wo_piece_load(i).wait()
+    for k, block in enumerate(others):
+        wo_rest_load(k, block).wait()
+    runs = ((0, 3), (3, 3), (6, 2), (8, 2), (10, 1))
+    for u, count in runs:
+        add_rows(o_own, wo, y_own, head_of(u), count, u == 0)
+        if u == 0:
+            for r in range(ends):
+                end_copy(r).start()
+    add_rows(o_own, wo, y_own, head_of(heads - 1), 1, False)
 
     pass_x(1)
-    for u in range(group):
-        o_copy(u).wait_recv()
-    add_rows(o_oth, w_oth, y_oth, group_of(0) * group, group, True)
-    for i in range(pieces):
-        hand_on(core_peer, i, d1_s, d1_r, at(core_peer)).wait_recv()
-    for u in range(group, 2 * group):
-        o_copy(u).wait_recv()
-    add_rows(o_oth, w_oth, y_oth, group_of(1) * group, group, False)
-    pass_x(2)
-    for u in range(2 * group, 3 * group):
-        o_copy(u).wait_recv()
-    add_rows(o_oth, w_oth, y_oth, group_of(2) * group, group, False)
-    for i in range(pieces):
-        hand_on(far_peer, i, d2_s, d2_r, at(core_peer)).wait_recv()
-    for u in range(3 * group, heads - 1):
-        o_copy(u).wait_recv()
-    add_rows(o_oth, w_oth, y_oth, last, group - 1, False)
-    o_copy(heads - 1).wait_recv()
-
-    def out_copy(c):
-        cols = pl.ds(pl.multiple_of(c * COLS, COLS), COLS)
-        return pltpu.make_async_copy(xbuf.at[:, cols], y_hbm.at[:, cols], out_sem.at[c])
-
-    def finish(c, carry):
-        h = last + group - 1
-        cols = pl.ds(pl.multiple_of(c * COLS, COLS), COLS)
-        part = jnp.dot(o_oth[h], w_oth[pl.ds(pl.multiple_of(h * HEAD, HEAD), HEAD), cols], preferred_element_type=F32)
-        xbuf[:, cols] = (y_own[:, cols] + (y_oth[:, cols] + part)).astype(BF16)
-        out_copy(c).start()
-        return carry
-
-    lax.fori_loop(0, n_cols, finish, 0)
+    for u, count in runs:
+        for k in range(u, u + count):
+            o_copy(k).wait_recv()
+        if u == 3:
+            for i in range(pieces):
+                hand_on(core_peer, i, d1_s, d1_r, at(core_peer)).wait_recv()
+        if u == 8:
+            for i in range(pieces - 1):
+                hand_on(far_peer, i, d2_s, d2_r, at(core_peer)).wait_recv()
+        if u == 10:
+            pass_x(2)
+        add_rows(o_oth, w_oth, y_oth, head_of(u), count, u == 0)
+    hand_on(far_peer, pieces - 1, d2_s, d2_r, at(core_peer)).wait_recv()
+
+    h_end = head_of(heads - 1)
+    w_end = pl.ds(pl.multiple_of(h_end * HEAD, HEAD), HEAD)
+    for r in range(ends):
+        rows = pl.ds(r * HEAD, HEAD)
+        end_copy(r).wait_recv()
+
+        for c in range(n_cols):
+            cols = pl.ds(c * COLS, COLS)
+            part = jnp.dot(o_oth[h_end, rows, :], w_oth[w_end, cols], preferred_element_type=F32)
+            y_out[rows, cols] = (y_own[rows, cols] + (y_oth[rows, cols] + part)).astype(BF16)
 
     for i in range(pieces):
         y_copy(i).wait_send()
         hand_on(me, i, xf_s, xf_r, at(chip_peer)).wait_send()
         hand_on(me, i, d1_s, d1_r, at(core_peer)).wait_send()
         hand_on(chip_peer, i, d2_s, d2_r, at(core_peer)).wait_send()
-    for k, block in enumerate((core_peer, chip_peer, far_peer)):
+    for k, block in enumerate(others):
         seg_copy(k, me, at(block)).wait_send()
     kv_copy(1, me, at(core_peer)).wait_send()
 
@@ -292,10 +315,10 @@
     def _():
         kv_copy(2, chip_peer, at(core_peer)).wait_send()
 
-    for u in range(heads):
+    for u in range(heads - 1):
         o_copy(u).wait_send()
-    for c in range(n_cols):
-        out_copy(c).wait()
+    for r in range(ends):
+        end_copy(r).wait_send()
 
 
 def solution(mesh):
@@ -310,9 +333,9 @@
         any_spec = pl.BlockSpec(memory_space=pl.ANY)
         return pl.pallas_call(
             layer_kernel,
-            out_shape=jax.ShapeDtypeStruct((chunk, width), BF16),
+            out_shape=pltpu.VMEM((chunk, width), BF16),
             in_specs=[any_spec] * 6,
-            out_specs=any_spec,
+            out_specs=pl.BlockSpec(memory_space=pltpu.VMEM),
             scratch_shapes=[
                 pltpu.VMEM((n_blocks, 1, chunk), jnp.int32),
                 pltpu.VMEM((chunk, HEAD), jnp.int32),
@@ -326,13 +349,13 @@
                 pltpu.VMEM(w_out.shape, BF16),
                 pltpu.VMEM((chunk, width), F32),
                 pltpu.VMEM((chunk, width), F32),
-                dma((3,)), dma((4,)), dma((width // COLS,)),
+                dma((5 + pieces,)), dma((4,)),
                 dma((3,)), dma((3,)), dma((3,)), dma((3,)),
                 dma((pieces,)), dma((pieces,)), dma((pieces,)), dma((pieces,)),
                 dma((pieces,)), dma((pieces,)), dma((pieces,)), dma((pieces,)),
-                dma((heads,)), dma((heads,)),
+                dma((heads - 1 + chunk // HEAD,)), dma((heads - 1 + chunk // HEAD,)),
             ],
-            compiler_params=pltpu.CompilerParams(collective_id=0, has_side_effects=True, vmem_limit_bytes=67043328),
+            compiler_params=pltpu.CompilerParams(collective_id=0, has_side_effects=True, vmem_limit_bytes=58 * 2 ** 20),
         )(seg_loc.reshape(1, chunk), x_loc, w_query, w_key, w_value, w_out)
 
     rows = P(('dp', 'cp'), None)

time: 97.2 us -> 94.2 us (0.969)
  local copies, waits for them, and re-layouts: 3.76 us -> 1.67 us
    unnamed x1, local copies, waits for them, and re-layouts: 3.76 us -> 1.67 us
where the time goes in v2:
time: 94.2 us; the launch traced here: 94.1 us
  Pallas kernels  92.4 us (98%)
  local copies, waits for them, and re-layouts  1.67 us (2%)
    pallas_call x1, Pallas kernels, layer(): pl.pallas_call(layer_kernel, out_shape=pltpu.VMEM((chunk, width), BF16),...  92.4 us

profile of v2, /device:TPU:0, one launch (start us, length us, event | category | flops | bytes accessed | tf_op | source)
XLA Modules:
  0.0 94.1 jit_solution(7664592102530697055)
XLA Ops:
  0.0 92.4 %shard_map.64 = bf16[512,3072]{1,0:T(8,128)(2,1)S(1)} custom-call(s32[1,512]{1,0:T(1,128)} %bitcast.1, bf16[512,3072]{1,0:T(8,128)(2,1)} %x_hbm.1, bf16[3072,1536]{1,0:T(8,128)(2,1)} %wq_hbm.1, bf16[3072,512]{1,0:T(8,128)(2,1)} %wk_hbm.1, bf16[3072,512]{1,0:T(8,128)(2,1)} %wv_hbm.1, bf16[1536,3072]{1,0:T(8,128)(2,1)} %wo_hbm.1), custom_call_target="tpu_custom_call" | custom-call | tf_op jit(solution)/shard_map/pallas_call | solution.py:334
  92.4 1.7 %copy.8 = bf16[512,3072]{1,0:T(8,128)(2,1)} copy(bf16[512,3072]{1,0:T(8,128)(2,1)S(1)} %shard_map.64) | data formatting | bytes 6291456

commit v3 on v2

--- a/solution.py
+++ b/solution.py
@@ -1,3 +1,4 @@
+import functools
 import math
 
 import jax
@@ -16,8 +17,9 @@
 SCALE = HEAD ** -0.5 * math.log2(math.e)
 
 
-def layer_kernel(seg_hbm, x_hbm, wq_hbm, wk_hbm, wv_hbm, wo_hbm, y_out,
-                 seg, segq, xbuf, wbuf, kv, q, o_own, o_oth, wo, w_oth, y_own, y_oth,
+def layer_kernel(seg_hbm, x_hbm, wq_hbm, wk_hbm, wv_hbm, wo_hbm,
+                 y_own, y_oth, o_oth, w_oth,
+                 seg, segq, xbuf, wbuf, kv, q, o_own, wo,
                  load_sem, tile_sem, seg_s, seg_r, kv_s, kv_r,
                  y_s, y_r, xf_s, xf_r, d1_s, d1_r, d2_s, d2_r, o_s, o_r):
     chunk, width = xbuf.shape
@@ -32,7 +34,6 @@
     kv_tiles = 2 * kv_heads * HEAD // TILE
     q_tiles = heads * HEAD // TILE
     slots = wbuf.shape[0]
-    ends = chunk // HEAD
 
     dp = lax.axis_index('dp')
     tp = lax.axis_index('tp')
@@ -40,6 +41,7 @@
     core_peer = me + 1 - 2 * lax.rem(me, 2)
     chip_peer = lax.rem(me + 2, 4)
     far_peer = 3 - me
+    others = (core_peer, chip_peer, far_peer)
     tp_peer = (dp, 1 - tp, me)
 
     def at(block):
@@ -49,6 +51,10 @@
         return pltpu.make_async_remote_copy(src_ref=src, dst_ref=dst, send_sem=s_sem, recv_sem=r_sem,
                                             device_id=where, device_id_type=MESH)
 
+    barrier = pltpu.get_barrier_semaphore()
+    for where in (tp_peer, at(core_peer), at(chip_peer), at(far_peer)):
+        pl.semaphore_signal(barrier, inc=1, device_id=where, device_id_type=MESH)
+
     def kv_tile_src(t):
         per = kv_tiles // 2
         return (wk_hbm if t < per else wv_hbm).at[:, pl.ds((t % per) * TILE, TILE)]
@@ -60,32 +66,21 @@
         return wq_hbm.at[:, pl.ds(pl.multiple_of(t * TILE, TILE), TILE)]
 
     x_load = pltpu.make_async_copy(x_hbm, xbuf, load_sem.at[0])
+    wo_load = pltpu.make_async_copy(wo_hbm, wo, load_sem.at[2])
     seg_load = pltpu.make_async_copy(seg_hbm, seg.at[me], load_sem.at[1])
 
-    def rows_of(block, i):
-        return pl.ds(pl.multiple_of(block * quarter + i * piece, piece), piece)
-
-    def wo_piece_load(i):
-        return pltpu.make_async_copy(wo_hbm.at[rows_of(me, i)], wo.at[rows_of(me, i)], load_sem.at[2 + i])
-
-    def wo_rest_load(k, block):
-        rows = pl.ds(pl.multiple_of(block * quarter, quarter), quarter)
-        return pltpu.make_async_copy(wo_hbm.at[rows], wo.at[rows], load_sem.at[2 + pieces + k])
-
-    others = (core_peer, chip_peer, far_peer)
-    wo_piece_load(0).start()
     x_load.start()
     for t in range(kv_tiles):
         tile_copy(kv_tile_src(t), t).start()
     seg_load.start()
 
-    barrier = pltpu.get_barrier_semaphore()
-    for where in (tp_peer, at(core_peer), at(chip_peer), at(far_peer)):
-        pl.semaphore_signal(barrier, inc=1, device_id=where, device_id_type=MESH)
     pl.semaphore_wait(barrier, 4)
 
+    def rows_of(block, i):
+        return pl.ds(pl.multiple_of(block * quarter + i * piece, piece), piece)
+
     def y_copy(i):
-        return remote((wo if i == 0 else wo_hbm).at[rows_of(me, i)], w_oth.at[rows_of(me, i)], y_s.at[i], y_r.at[i], tp_peer)
+        return remote(wo_hbm.at[rows_of(me, i)], w_oth.at[rows_of(me, i)], y_s.at[i], y_r.at[i], tp_peer)
 
     def hand_on(block, i, s_sem, r_sem, where):
         part = w_oth.at[rows_of(block, i)]
@@ -101,11 +96,6 @@
     def o_copy(u):
         h = head_of(u)
         return remote(o_own.at[h], o_oth.at[h], o_s.at[u], o_r.at[u], tp_peer)
-
-    def end_copy(r):
-        h = head_of(heads - 1)
-        rows = pl.ds(r * HEAD, HEAD)
-        return remote(o_own.at[h, rows], o_oth.at[h, rows], o_s.at[heads - 1 + r], o_r.at[heads - 1 + r], tp_peer)
 
     def group_of(j):
         high = lax.rem(me // 2 + j // 2, 2)
@@ -124,7 +114,6 @@
         j, i = place_of(u)
         return group_of(j) * group + i
 
-    wo_piece_load(0).wait()
     for i in range(pieces):
         y_copy(i).start()
     seg_load.wait()
@@ -164,10 +153,7 @@
             def _():
                 kv_copy(0, me, at(chip_peer)).start()
             kv_copy(1, me, at(core_peer)).start()
-            for i in range(1, pieces):
-                wo_piece_load(i).start()
-            for k, block in enumerate(others):
-                wo_rest_load(k, block).start()
+            wo_load.start()
         return 0
 
     lax.fori_loop(0, q_tiles, project_q, 0)
@@ -260,16 +246,12 @@
 
         lax.fori_loop(0, n_cols, one, 0)
 
-    for i in range(1, pieces):
-        wo_piece_load(i).wait()
-    for k, block in enumerate(others):
-        wo_rest_load(k, block).wait()
+    wo_load.wait()
     runs = ((0, 3), (3, 3), (6, 2), (8, 2), (10, 1))
     for u, count in runs:
         add_rows(o_own, wo, y_own, head_of(u), count, u == 0)
         if u == 0:
-            for r in range(ends):
-                end_copy(r).start()
+            o_copy(heads - 1).start()
     add_rows(o_own, wo, y_own, head_of(heads - 1), 1, False)
 
     pass_x(1)
@@ -287,16 +269,7 @@
         add_rows(o_oth, w_oth, y_oth, head_of(u), count, u == 0)
     hand_on(far_peer, pieces - 1, d2_s, d2_r, at(core_peer)).wait_recv()
 
-    h_end = head_of(heads - 1)
-    w_end = pl.ds(pl.multiple_of(h_end * HEAD, HEAD), HEAD)
-    for r in range(ends):
-        rows = pl.ds(r * HEAD, HEAD)
-        end_copy(r).wait_recv()
-
-        for c in range(n_cols):
-            cols = pl.ds(c * COLS, COLS)
-            part = jnp.dot(o_oth[h_end, rows, :], w_oth[w_end, cols], preferred_element_type=F32)
-            y_out[rows, cols] = (y_own[rows, cols] + (y_oth[rows, cols] + part)).astype(BF16)
+    o_copy(heads - 1).wait_recv()
 
     for i in range(pieces):
         y_copy(i).wait_send()
@@ -315,10 +288,24 @@
     def _():
         kv_copy(2, chip_peer, at(core_peer)).wait_send()
 
-    for u in range(heads - 1):
+    for u in range(heads):
         o_copy(u).wait_send()
-    for r in range(ends):
-        end_copy(r).wait_send()
+
+
+def last_kernel(last_head, y_own, y_oth, o_oth, w_oth, y_hbm, y_out, out_sem):
+    h = last_head(lax.axis_index('cp'))
+    left = o_oth[h]
+    rows = pl.ds(pl.multiple_of(h * HEAD, HEAD), HEAD)
+    copies = []
+    for c in range(y_out.shape[1] // COLS):
+        cols = pl.ds(c * COLS, COLS)
+        part = jnp.dot(left, w_oth[rows, cols], preferred_element_type=F32)
+        y_out[:, cols] = (y_own[:, cols] + (y_oth[:, cols] + part)).astype(BF16)
+        copy = pltpu.make_async_copy(y_out.at[:, cols], y_hbm.at[:, cols], out_sem.at[c])
+        copy.start()
+        copies.append(copy)
+    for copy in copies:
+        copy.wait()
 
 
 def solution(mesh):
@@ -331,11 +318,17 @@
         pieces = 3
         dma = pltpu.SemaphoreType.DMA
         any_spec = pl.BlockSpec(memory_space=pl.ANY)
-        return pl.pallas_call(
+        vmem_spec = pl.BlockSpec(memory_space=pltpu.VMEM)
+        parts = pl.pallas_call(
             layer_kernel,
-            out_shape=pltpu.VMEM((chunk, width), BF16),
+            out_shape=(
+                pltpu.VMEM((chunk, width), F32),
+                pltpu.VMEM((chunk, width), F32),
+                pltpu.VMEM((heads, chunk, HEAD), BF16),
+                pltpu.VMEM(w_out.shape, BF16),
+            ),
             in_specs=[any_spec] * 6,
-            out_specs=pl.BlockSpec(memory_space=pltpu.VMEM),
+            out_specs=[vmem_spec] * 4,
             scratch_shapes=[
                 pltpu.VMEM((n_blocks, 1, chunk), jnp.int32),
                 pltpu.VMEM((chunk, HEAD), jnp.int32),
@@ -344,19 +337,28 @@
                 pltpu.VMEM((2 * kv_heads, n_blocks * chunk, HEAD), BF16),
                 pltpu.VMEM((heads, chunk, HEAD), BF16),
                 pltpu.VMEM((heads, chunk, HEAD), BF16),
-                pltpu.VMEM((heads, chunk, HEAD), BF16),
                 pltpu.VMEM(w_out.shape, BF16),
-                pltpu.VMEM(w_out.shape, BF16),
-                pltpu.VMEM((chunk, width), F32),
-                pltpu.VMEM((chunk, width), F32),
-                dma((5 + pieces,)), dma((4,)),
+                dma((3,)), dma((4,)),
                 dma((3,)), dma((3,)), dma((3,)), dma((3,)),
                 dma((pieces,)), dma((pieces,)), dma((pieces,)), dma((pieces,)),
                 dma((pieces,)), dma((pieces,)), dma((pieces,)), dma((pieces,)),
-                dma((heads - 1 + chunk // HEAD,)), dma((heads - 1 + chunk // HEAD,)),
+                dma((heads,)), dma((heads,)),
             ],
-            compiler_params=pltpu.CompilerParams(collective_id=0, has_side_effects=True, vmem_limit_bytes=58 * 2 ** 20),
+            compiler_params=pltpu.CompilerParams(collective_id=0, has_side_effects=True, vmem_limit_bytes=36 * 2 ** 20),
         )(seg_loc.reshape(1, chunk), x_loc, w_query, w_key, w_value, w_out)
+        parts = [pltpu.with_memory_space_constraint(a, pltpu.VMEM) for a in parts]
+
+        def last_head(me):
+            return (3 - me) * (heads // kv_heads) + heads // kv_heads - 1
+
+        return pl.pallas_call(
+            functools.partial(last_kernel, last_head),
+            out_shape=jax.ShapeDtypeStruct((chunk, width), BF16),
+            in_specs=[vmem_spec] * 4,
+            out_specs=any_spec,
+            scratch_shapes=[pltpu.VMEM((chunk, width), BF16), dma((width // COLS,))],
+            compiler_params=pltpu.CompilerParams(vmem_limit_bytes=8 * 2 ** 20),
+        )(*parts)
 
     rows = P(('dp', 'cp'), None)
     return jax.shard_map(layer, mesh=mesh,

time: 94.2 us -> 92.9 us (0.986)
  local copies, waits for them, and re-layouts: 1.67 us -> 0 us
    unnamed x1 -> x0, local copies, waits for them, and re-layouts: 1.67 us -> none
    pallas_call x1 -> x2, Pallas kernels: 92.4 us -> 92.7 us  [the longest x1 90.7 us: layer(): pl.pallas_call(layer_kernel, out_shape=(pltpu.VMEM((chunk, width), F32),...]
where the time goes in v3:
time: 92.9 us; the launch traced here: 92.8 us
  Pallas kernels  92.7 us (100%)
    pallas_call x1, Pallas kernels, layer(): pl.pallas_call(layer_kernel, out_shape=(pltpu.VMEM((chunk, width), F32),...  90.7 us
    pallas_call x1, Pallas kernels, layer(): pl.pallas_call(functools.partial(last_kernel, last_head), out_shape=jax.S...  2.01 us

profile of v3, /device:TPU:0, one launch (start us, length us, event | category | flops | bytes accessed | tf_op | source)
XLA Modules:
  0.0 92.8 jit_solution(4583903022156531059)
XLA Ops:
  0.0 90.7 %shard_map.64 = (f32[512,3072]{1,0:T(8,128)S(1)}, f32[512,3072]{1,0:T(8,128)S(1)}, bf16[12,512,128]{2,1,0:T(8,128)(2,1)S(1)}, bf16[1536,3072]{1,0:T(8,128)(2,1)S(1)}) custom-call(s32[1,512]{1,0:T(1,128)} %bitcast.1, bf16[512,3072]{1,0:T(8,128)(2,1)} %x_hbm.1, bf16[3072,1536]{1,0:T(8,128)(2,1)} %wq_hbm.1, bf16[3072,512]{1,0:T(8,128)(2,1)} %wk_hbm.1, ...), custom_call_target="tpu_custom_call" | custom-call | tf_op jit(solution)/shard_map/pallas_call | solution.py:322
  90.7 2.0 %shard_map.65 = bf16[512,3072]{1,0:T(8,128)(2,1)} custom-call(f32[512,3072]{1,0:T(8,128)S(1)} %get-tuple-element.9.y_own, f32[512,3072]{1,0:T(8,128)S(1)} %get-tuple-element.10.y_oth, bf16[12,512,128]{2,1,0:T(8,128)(2,1)S(1)} %get-tuple-element.11.o_oth, bf16[1536,3072]{1,0:T(8,128)(2,1)S(1)} %get-tuple-element.12.w_oth), custom_call_target="tpu_custom_call" | custom-call | tf_op jit(solution)/shard_map/pallas_call | solution.py:354

commit v4 on v3

--- a/solution.py
+++ b/solution.py
@@ -20,7 +20,7 @@
 def layer_kernel(seg_hbm, x_hbm, wq_hbm, wk_hbm, wv_hbm, wo_hbm,
                  y_own, y_oth, o_oth, w_oth,
                  seg, segq, xbuf, wbuf, kv, q, o_own, wo,
-                 load_sem, tile_sem, seg_s, seg_r, kv_s, kv_r,
+                 entry, load_sem, tile_sem, seg_s, seg_r, kv_s, kv_r,
                  y_s, y_r, xf_s, xf_r, d1_s, d1_r, d2_s, d2_r, o_s, o_r):
     chunk, width = xbuf.shape
     kv_heads = kv.shape[0] // 2
@@ -51,9 +51,14 @@
         return pltpu.make_async_remote_copy(src_ref=src, dst_ref=dst, send_sem=s_sem, recv_sem=r_sem,
                                             device_id=where, device_id_type=MESH)
 
+    odd = lax.rem(me, 2)
     barrier = pltpu.get_barrier_semaphore()
-    for where in (tp_peer, at(core_peer), at(chip_peer), at(far_peer)):
+    for where in (tp_peer, at(core_peer)):
         pl.semaphore_signal(barrier, inc=1, device_id=where, device_id_type=MESH)
+
+    @pl.when(odd == 1)
+    def _():
+        pl.semaphore_signal(barrier, inc=1, device_id=at(chip_peer), device_id_type=MESH)
 
     def kv_tile_src(t):
         per = kv_tiles // 2
@@ -74,7 +79,6 @@
         tile_copy(kv_tile_src(t), t).start()
     seg_load.start()
 
-    pl.semaphore_wait(barrier, 4)
 
     def rows_of(block, i):
         return pl.ds(pl.multiple_of(block * quarter + i * piece, piece), piece)
@@ -114,8 +118,20 @@
         j, i = place_of(u)
         return group_of(j) * group + i
 
+    pl.semaphore_wait(barrier, 2 + odd)
     for i in range(pieces):
         y_copy(i).start()
+
+    @pl.when(odd == 1)
+    def _():
+        pl.semaphore_signal(entry, inc=1, device_id=at(chip_peer), device_id_type=MESH)
+        pl.semaphore_wait(entry, 1)
+        pl.semaphore_signal(entry, inc=1, device_id=at(core_peer), device_id_type=MESH)
+
+    @pl.when(odd == 0)
+    def _():
+        pl.semaphore_wait(entry, 1)
+
     seg_load.wait()
     for k, block in enumerate(others):
         seg_copy(k, me, at(block)).start()
@@ -338,7 +354,7 @@
                 pltpu.VMEM((heads, chunk, HEAD), BF16),
                 pltpu.VMEM((heads, chunk, HEAD), BF16),
                 pltpu.VMEM(w_out.shape, BF16),
-                dma((3,)), dma((4,)),
+                pltpu.SemaphoreType.REGULAR, dma((3,)), dma((4,)),
                 dma((3,)), dma((3,)), dma((3,)), dma((3,)),
                 dma((pieces,)), dma((pieces,)), dma((pieces,)), dma((pieces,)),
                 dma((pieces,)), dma((pieces,)), dma((pieces,)), dma((pieces,)),

time: 92.9 us -> 91.6 us (0.986)
  Pallas kernels: 92.7 us -> 91.5 us
    pallas_call x1, Pallas kernels: 90.7 us -> 89.5 us  [layer(): pl.pallas_call(layer_kernel, out_shape=(pltpu.VMEM((chunk, width), F32),...]
where the time goes in v4:
time: 91.6 us; the launch traced here: 91.5 us
  Pallas kernels  91.5 us (100%)
    pallas_call x1, Pallas kernels, layer(): pl.pallas_call(layer_kernel, out_shape=(pltpu.VMEM((chunk, width), F32),...  89.5 us
    pallas_call x1, Pallas kernels, layer(): pl.pallas_call(functools.partial(last_kernel, last_head), out_shape=jax.S...  2 us

profile of v4, /device:TPU:0, one launch (start us, length us, event | category | flops | bytes accessed | tf_op | source)
XLA Modules:
  0.0 91.5 jit_solution(1789642837374084718)
XLA Ops:
  0.0 89.5 %shard_map.64 = (f32[512,3072]{1,0:T(8,128)S(1)}, f32[512,3072]{1,0:T(8,128)S(1)}, bf16[12,512,128]{2,1,0:T(8,128)(2,1)S(1)}, bf16[1536,3072]{1,0:T(8,128)(2,1)S(1)}) custom-call(s32[1,512]{1,0:T(1,128)} %bitcast.1, bf16[512,3072]{1,0:T(8,128)(2,1)} %x_hbm.1, bf16[3072,1536]{1,0:T(8,128)(2,1)} %wq_hbm.1, bf16[3072,512]{1,0:T(8,128)(2,1)} %wk_hbm.1, ...), custom_call_target="tpu_custom_call" | custom-call | tf_op jit(solution)/shard_map/pallas_call | solution.py:338
  89.5 2.0 %shard_map.65 = bf16[512,3072]{1,0:T(8,128)(2,1)} custom-call(f32[512,3072]{1,0:T(8,128)S(1)} %get-tuple-element.9.y_own, f32[512,3072]{1,0:T(8,128)S(1)} %get-tuple-element.10.y_oth, bf16[12,512,128]{2,1,0:T(8,128)(2,1)S(1)} %get-tuple-element.11.o_oth, bf16[1536,3072]{1,0:T(8,128)(2,1)S(1)} %get-tuple-element.12.w_oth), custom_call_target="tpu_custom_call" | custom-call | tf_op jit(solution)/shard_map/pallas_call | solution.py:370

commit v5 on v4

--- a/solution.py
+++ b/solution.py
@@ -11,6 +11,7 @@
 HEAD = 128
 TILE = 256
 COLS = 512
+SENDS = ((0, 3), (3, 3), (6, 2), (8, 2), (10, 1), (11, 1))
 MESH = pl.DeviceIdType.MESH
 F32 = jnp.float32
 BF16 = jnp.bfloat16
@@ -97,9 +98,9 @@
         part = kv.at[:, pl.ds(pl.multiple_of(block * chunk, chunk), chunk), :]
         return remote(part, part, kv_s.at[k], kv_r.at[k], where)
 
-    def o_copy(u):
-        h = head_of(u)
-        return remote(o_own.at[h], o_oth.at[h], o_s.at[u], o_r.at[u], tp_peer)
+    def o_copy(k):
+        part = pl.ds(*SENDS[k])
+        return remote(o_own.at[part], o_oth.at[part], o_s.at[k], o_r.at[k], tp_peer)
 
     def group_of(j):
         high = lax.rem(me // 2 + j // 2, 2)
@@ -197,7 +198,7 @@
         kv_copy(2, chip_peer, at(core_peer)).start()
         kv_copy(2, far_peer, at(core_peer)).wait_recv()
 
-    def attend(h, g, r, n):
+    def attend(u, h, g, r, n):
         rows = pl.ds(pl.multiple_of(r * TILE, TILE), TILE)
         q_t = q[h, rows, :]
         sq = segq[rows, :]
@@ -221,7 +222,7 @@
             pv = jnp.dot(p.astype(BF16), kv[kv_heads + g, pl.ds(b * chunk, chunk), :], preferred_element_type=F32)
             total = row_sum if total is None else total + row_sum
             acc = pv if acc is None else acc + pv
-        o_own[h, rows, :] = (acc / total).astype(BF16)
+        o_own[u, rows, :] = (acc / total).astype(BF16)
 
     def attend_head(u, _):
         h = head_of(u)
@@ -230,13 +231,14 @@
             @pl.when(me == n - 1)
             def _(n=n):
                 def one(r, c):
-                    attend(h, g, r, n)
+                    attend(u, h, g, r, n)
                     return c
                 lax.fori_loop(0, chunk // TILE, one, 0)
 
-        @pl.when(u > 0)
-        def _():
-            o_copy(u - 1).start()
+        for k, (begin, count) in enumerate(SENDS[:-1]):
+            @pl.when(u == begin + count)
+            def _(k=k):
+                o_copy(k).start()
 
         @pl.when(u == group - 1)
         def _():
@@ -250,12 +252,12 @@
     lax.fori_loop(0, heads, attend_head, 0)
     pass_y(2)
 
-    def add_rows(o_ref, w_ref, y_ref, h0, count, first):
-        rows = pl.ds(pl.multiple_of(h0 * HEAD, HEAD), count * HEAD)
+    def add_rows(o_ref, w_ref, y_ref, u, count, first):
+        rows = pl.ds(pl.multiple_of(head_of(u) * HEAD, HEAD), count * HEAD)
 
         def one(c, carry):
             cols = pl.ds(pl.multiple_of(c * COLS, COLS), COLS)
-            left = jnp.concatenate([o_ref[h0 + k] for k in range(count)], axis=1)
+            left = jnp.concatenate([o_ref[u + k] for k in range(count)], axis=1)
             part = jnp.dot(left, w_ref[rows, cols], preferred_element_type=F32)
             y_ref[:, cols] = part if first else y_ref[:, cols] + part
             return carry
@@ -265,15 +267,16 @@
     wo_load.wait()
     runs = ((0, 3), (3, 3), (6, 2), (8, 2), (10, 1))
     for u, count in runs:
-        add_rows(o_own, wo, y_own, head_of(u), count, u == 0)
+        add_rows(o_own, wo, y_own, u, count, u == 0)
         if u == 0:
-            o_copy(heads - 1).start()
-    add_rows(o_own, wo, y_own, head_of(heads - 1), 1, False)
+            o_copy(len(SENDS) - 1).start()
+    add_rows(o_own, wo, y_own, heads - 1, 1, False)
 
     pass_x(1)
     for u, count in runs:
-        for k in range(u, u + count):
-            o_copy(k).wait_recv()
+        for k, (begin, _) in enumerate(SENDS):
+            if u <= begin < u + count:
+                o_copy(k).wait_recv()
         if u == 3:
             for i in range(pieces):
                 hand_on(core_peer, i, d1_s, d1_r, at(core_peer)).wait_recv()
@@ -282,10 +285,10 @@
                 hand_on(far_peer, i, d2_s, d2_r, at(core_peer)).wait_recv()
         if u == 10:
             pass_x(2)
-        add_rows(o_oth, w_oth, y_oth, head_of(u), count, u == 0)
+        add_rows(o_oth, w_oth, y_oth, u, count, u == 0)
     hand_on(far_peer, pieces - 1, d2_s, d2_r, at(core_peer)).wait_recv()
 
-    o_copy(heads - 1).wait_recv()
+    o_copy(len(SENDS) - 1).wait_recv()
 
     for i in range(pieces):
         y_copy(i).wait_send()
@@ -304,13 +307,13 @@
     def _():
         kv_copy(2, chip_peer, at(core_peer)).wait_send()
 
-    for u in range(heads):
-        o_copy(u).wait_send()
+    for k in range(len(SENDS)):
+        o_copy(k).wait_send()
 
 
 def last_kernel(last_head, y_own, y_oth, o_oth, w_oth, y_hbm, y_out, out_sem):
     h = last_head(lax.axis_index('cp'))
-    left = o_oth[h]
+    left = o_oth[o_oth.shape[0] - 1]
     rows = pl.ds(pl.multiple_of(h * HEAD, HEAD), HEAD)
     copies = []
     for c in range(y_out.shape[1] // COLS):
@@ -358,7 +361,7 @@
                 dma((3,)), dma((3,)), dma((3,)), dma((3,)),
                 dma((pieces,)), dma((pieces,)), dma((pieces,)), dma((pieces,)),
                 dma((pieces,)), dma((pieces,)), dma((pieces,)), dma((pieces,)),
-                dma((heads,)), dma((heads,)),
+                dma((len(SENDS),)), dma((len(SENDS),)),
             ],
             compiler_params=pltpu.CompilerParams(collective_id=0, has_side_effects=True, vmem_limit_bytes=36 * 2 ** 20),
         )(seg_loc.reshape(1, chunk), x_loc, w_query, w_key, w_value, w_out)

time: 91.6 us -> 91.5 us (level)
  no operation moved by 1% of the time
where the time goes in v5:
time: 91.5 us; the launch traced here: 91.4 us
  Pallas kernels  91.4 us (100%)
    pallas_call x1, Pallas kernels, layer(): pl.pallas_call(layer_kernel, out_shape=(pltpu.VMEM((chunk, width), F32),...  89.4 us
    pallas_call x1, Pallas kernels, layer(): pl.pallas_call(functools.partial(last_kernel, last_head), out_shape=jax.S...  2 us

profile of v5, /device:TPU:0, one launch (start us, length us, event | category | flops | bytes accessed | tf_op | source)
XLA Modules:
  0.0 91.4 jit_solution(107750062282243356)
XLA Ops:
  0.0 89.4 %shard_map.64 = (f32[512,3072]{1,0:T(8,128)S(1)}, f32[512,3072]{1,0:T(8,128)S(1)}, bf16[12,512,128]{2,1,0:T(8,128)(2,1)S(1)}, bf16[1536,3072]{1,0:T(8,128)(2,1)S(1)}) custom-call(s32[1,512]{1,0:T(1,128)} %bitcast.1, bf16[512,3072]{1,0:T(8,128)(2,1)} %x_hbm.1, bf16[3072,1536]{1,0:T(8,128)(2,1)} %wq_hbm.1, bf16[3072,512]{1,0:T(8,128)(2,1)} %wk_hbm.1, ...), custom_call_target="tpu_custom_call" | custom-call | tf_op jit(solution)/shard_map/pallas_call | solution.py:341
  89.4 2.0 %shard_map.65 = bf16[512,3072]{1,0:T(8,128)(2,1)} custom-call(f32[512,3072]{1,0:T(8,128)S(1)} %get-tuple-element.9.y_own, f32[512,3072]{1,0:T(8,128)S(1)} %get-tuple-element.10.y_oth, bf16[12,512,128]{2,1,0:T(8,128)(2,1)S(1)} %get-tuple-element.11.o_oth, bf16[1536,3072]{1,0:T(8,128)(2,1)S(1)} %get-tuple-element.12.w_oth), custom_call_target="tpu_custom_call" | custom-call | tf_op jit(solution)/shard_map/pallas_call | solution.py:373

commit v6 on v5

--- a/solution.py
+++ b/solution.py
@@ -11,6 +11,7 @@
 HEAD = 128
 TILE = 256
 COLS = 512
+EXTRA = 8
 SENDS = ((0, 3), (3, 3), (6, 2), (8, 2), (10, 1), (11, 1))
 MESH = pl.DeviceIdType.MESH
 F32 = jnp.float32
@@ -81,14 +82,27 @@
     seg_load.start()
 
 
-    def rows_of(block, i):
-        return pl.ds(pl.multiple_of(block * quarter + i * piece, piece), piece)
-
-    def y_copy(i):
-        return remote(wo_hbm.at[rows_of(me, i)], w_oth.at[rows_of(me, i)], y_s.at[i], y_r.at[i], tp_peer)
-
-    def hand_on(block, i, s_sem, r_sem, where):
-        part = w_oth.at[rows_of(block, i)]
+    def rows_of(block, i, moved):
+        begin = -EXTRA if moved and i == 0 else 0
+        end = -EXTRA if moved and i == pieces - 1 else 0
+        return pl.ds(pl.multiple_of(block * quarter + i * piece + begin, 8), piece - begin + end)
+
+    def by_piece(block, i, side, act):
+        if 0 < i < pieces - 1:
+            act(False)
+            return
+        edge = ((block == 2) if i == 0 else (block == 1)) & (side == 0)
+        for moved in (False, True):
+            @pl.when(edge if moved else jnp.logical_not(edge))
+            def _(moved=moved):
+                act(moved)
+
+    def y_copy(i, moved):
+        rows = rows_of(me, i, moved)
+        return remote(wo_hbm.at[rows], w_oth.at[rows], y_s.at[i], y_r.at[i], tp_peer)
+
+    def hand_on(block, i, moved, s_sem, r_sem, where):
+        part = w_oth.at[rows_of(block, i, moved)]
         return remote(part, part, s_sem.at[i], r_sem.at[i], where)
 
     def seg_copy(k, block, where):
@@ -121,7 +135,7 @@
 
     pl.semaphore_wait(barrier, 2 + odd)
     for i in range(pieces):
-        y_copy(i).start()
+        by_piece(me, i, 1 - tp, lambda moved, i=i: y_copy(i, moved).start())
 
     @pl.when(odd == 1)
     def _():
@@ -176,13 +190,23 @@
     lax.fori_loop(0, q_tiles, project_q, 0)
 
     def pass_y(i):
-        y_copy(i).wait_recv()
-        hand_on(me, i, xf_s, xf_r, at(chip_peer)).start()
-        hand_on(me, i, d1_s, d1_r, at(core_peer)).start()
+        def act(moved):
+            y_copy(i, moved).wait_recv()
+            hand_on(me, i, moved, xf_s, xf_r, at(chip_peer)).start()
+            hand_on(me, i, moved, d1_s, d1_r, at(core_peer)).start()
+        by_piece(me, i, tp, act)
 
     def pass_x(i):
-        hand_on(chip_peer, i, xf_s, xf_r, at(chip_peer)).wait_recv()
-        hand_on(chip_peer, i, d2_s, d2_r, at(core_peer)).start()
+        def act(moved):
+            hand_on(chip_peer, i, moved, xf_s, xf_r, at(chip_peer)).wait_recv()
+            hand_on(chip_peer, i, moved, d2_s, d2_r, at(core_peer)).start()
+        by_piece(chip_peer, i, tp, act)
+
+    def wait_near(i):
+        by_piece(core_peer, i, tp, lambda moved: hand_on(core_peer, i, moved, d1_s, d1_r, at(core_peer)).wait_recv())
+
+    def wait_far(i):
+        by_piece(far_peer, i, tp, lambda moved: hand_on(far_peer, i, moved, d2_s, d2_r, at(core_peer)).wait_recv())
 
     pass_y(0)
     for k, block in enumerate(others):
@@ -277,24 +301,28 @@
         for k, (begin, _) in enumerate(SENDS):
             if u <= begin < u + count:
                 o_copy(k).wait_recv()
+        if u == 0:
+            wait_far(0)
         if u == 3:
             for i in range(pieces):
-                hand_on(core_peer, i, d1_s, d1_r, at(core_peer)).wait_recv()
+                wait_near(i)
         if u == 8:
-            for i in range(pieces - 1):
-                hand_on(far_peer, i, d2_s, d2_r, at(core_peer)).wait_recv()
+            for i in range(1, pieces - 1):
+                wait_far(i)
         if u == 10:
             pass_x(2)
         add_rows(o_oth, w_oth, y_oth, u, count, u == 0)
-    hand_on(far_peer, pieces - 1, d2_s, d2_r, at(core_peer)).wait_recv()
+    wait_far(pieces - 1)
 
     o_copy(len(SENDS) - 1).wait_recv()
 
     for i in range(pieces):
-        y_copy(i).wait_send()
-        hand_on(me, i, xf_s, xf_r, at(chip_peer)).wait_send()
-        hand_on(me, i, d1_s, d1_r, at(core_peer)).wait_send()
-        hand_on(chip_peer, i, d2_s, d2_r, at(core_peer)).wait_send()
+        def sent(moved, i=i):
+            hand_on(me, i, moved, xf_s, xf_r, at(chip_peer)).wait_send()
+            hand_on(me, i, moved, d1_s, d1_r, at(core_peer)).wait_send()
+        by_piece(me, i, 1 - tp, lambda moved, i=i: y_copy(i, moved).wait_send())
+        by_piece(me, i, tp, sent)
+        by_piece(chip_peer, i, tp, lambda moved, i=i: hand_on(chip_peer, i, moved, d2_s, d2_r, at(core_peer)).wait_send())
     for k, block in enumerate(others):
         seg_copy(k, me, at(block)).wait_send()
     kv_copy(1, me, at(core_peer)).wait_send()

time: 91.5 us -> 91.3 us (level)
  no operation moved by 1% of the time
where the time goes in v6:
time: 91.3 us; the launch traced here: 91.2 us
  Pallas kernels  91.2 us (100%)
    pallas_call x1, Pallas kernels, layer(): pl.pallas_call(layer_kernel, out_shape=(pltpu.VMEM((chunk, width), F32),...  89.2 us
    pallas_call x1, Pallas kernels, layer(): pl.pallas_call(functools.partial(last_kernel, last_head), out_shape=jax.S...  2.01 us

profile of v6, /device:TPU:0, one launch (start us, length us, event | category | flops | bytes accessed | tf_op | source)
XLA Modules:
  0.0 91.2 jit_solution(17166459131701172443)
XLA Ops:
  0.0 89.2 %shard_map.64 = (f32[512,3072]{1,0:T(8,128)S(1)}, f32[512,3072]{1,0:T(8,128)S(1)}, bf16[12,512,128]{2,1,0:T(8,128)(2,1)S(1)}, bf16[1536,3072]{1,0:T(8,128)(2,1)S(1)}) custom-call(s32[1,512]{1,0:T(1,128)} %bitcast.1, bf16[512,3072]{1,0:T(8,128)(2,1)} %x_hbm.1, bf16[3072,1536]{1,0:T(8,128)(2,1)} %wq_hbm.1, bf16[3072,512]{1,0:T(8,128)(2,1)} %wk_hbm.1, ...), custom_call_target="tpu_custom_call" | custom-call | tf_op jit(solution)/shard_map/pallas_call | solution.py:369
  89.2 2.0 %shard_map.65 = bf16[512,3072]{1,0:T(8,128)(2,1)} custom-call(f32[512,3072]{1,0:T(8,128)S(1)} %get-tuple-element.9.y_own, f32[512,3072]{1,0:T(8,128)S(1)} %get-tuple-element.10.y_oth, bf16[12,512,128]{2,1,0:T(8,128)(2,1)S(1)} %get-tuple-element.11.o_oth, bf16[1536,3072]{1,0:T(8,128)(2,1)S(1)} %get-tuple-element.12.w_oth), custom_call_target="tpu_custom_call" | custom-call | tf_op jit(solution)/shard_map/pallas_call | solution.py:401

commit v7 on v6

--- a/solution.py
+++ b/solution.py
@@ -11,7 +11,9 @@
 HEAD = 128
 TILE = 256
 COLS = 512
-EXTRA = 8
+EXTRA = 16
+EARLY = (2, 3)
+SHORT = (1, 2)
 SENDS = ((0, 3), (3, 3), (6, 2), (8, 2), (10, 1), (11, 1))
 MESH = pl.DeviceIdType.MESH
 F32 = jnp.float32
@@ -91,7 +93,8 @@
         if 0 < i < pieces - 1:
             act(False)
             return
-        edge = ((block == 2) if i == 0 else (block == 1)) & (side == 0)
+        low, high = EARLY if i == 0 else SHORT
+        edge = (block >= low) & (block <= high) & (side == 0)
         for moved in (False, True):
             @pl.when(edge if moved else jnp.logical_not(edge))
             def _(moved=moved):
@@ -302,9 +305,10 @@
             if u <= begin < u + count:
                 o_copy(k).wait_recv()
         if u == 0:
+            wait_near(0)
             wait_far(0)
         if u == 3:
-            for i in range(pieces):
+            for i in range(1, pieces):
                 wait_near(i)
         if u == 8:
             for i in range(1, pieces - 1):

time: 91.3 us -> 90.8 us (level)
  no operation moved by 1% of the time
where the time goes in v7:
time: 90.8 us; the launch traced here: 90.7 us
  Pallas kernels  90.7 us (100%)
    pallas_call x1, Pallas kernels, layer(): pl.pallas_call(layer_kernel, out_shape=(pltpu.VMEM((chunk, width), F32),...  88.7 us
    pallas_call x1, Pallas kernels, layer(): pl.pallas_call(functools.partial(last_kernel, last_head), out_shape=jax.S...  2 us

profile of v7, /device:TPU:0, one launch (start us, length us, event | category | flops | bytes accessed | tf_op | source)
XLA Modules:
  0.0 90.7 jit_solution(3179835508660210218)
XLA Ops:
  0.0 88.7 %shard_map.64 = (f32[512,3072]{1,0:T(8,128)S(1)}, f32[512,3072]{1,0:T(8,128)S(1)}, bf16[12,512,128]{2,1,0:T(8,128)(2,1)S(1)}, bf16[1536,3072]{1,0:T(8,128)(2,1)S(1)}) custom-call(s32[1,512]{1,0:T(1,128)} %bitcast.1, bf16[512,3072]{1,0:T(8,128)(2,1)} %x_hbm.1, bf16[3072,1536]{1,0:T(8,128)(2,1)} %wq_hbm.1, bf16[3072,512]{1,0:T(8,128)(2,1)} %wk_hbm.1, ...), custom_call_target="tpu_custom_call" | custom-call | tf_op jit(solution)/shard_map/pallas_call | solution.py:373
  88.7 2.0 %shard_map.65 = bf16[512,3072]{1,0:T(8,128)(2,1)} custom-call(f32[512,3072]{1,0:T(8,128)S(1)} %get-tuple-element.9.y_own, f32[512,3072]{1,0:T(8,128)S(1)} %get-tuple-element.10.y_oth, bf16[12,512,128]{2,1,0:T(8,128)(2,1)S(1)} %get-tuple-element.11.o_oth, bf16[1536,3072]{1,0:T(8,128)(2,1)S(1)} %get-tuple-element.12.w_oth), custom_call_target="tpu_custom_call" | custom-call | tf_op jit(solution)/shard_map/pallas_call | solution.py:405

commit v8 on v7

--- a/solution.py
+++ b/solution.py
@@ -57,8 +57,11 @@
 
     odd = lax.rem(me, 2)
     barrier = pltpu.get_barrier_semaphore()
-    for where in (tp_peer, at(core_peer)):
-        pl.semaphore_signal(barrier, inc=1, device_id=where, device_id_type=MESH)
+    pl.semaphore_signal(barrier, inc=1, device_id=tp_peer, device_id_type=MESH)
+
+    @pl.when(odd == 0)
+    def _():
+        pl.semaphore_signal(barrier, inc=1, device_id=at(core_peer), device_id_type=MESH)
 
     @pl.when(odd == 1)
     def _():
@@ -136,7 +139,7 @@
         j, i = place_of(u)
         return group_of(j) * group + i
 
-    pl.semaphore_wait(barrier, 2 + odd)
+    pl.semaphore_wait(barrier, 1 + 2 * odd)
     for i in range(pieces):
         by_piece(me, i, 1 - tp, lambda moved, i=i: y_copy(i, moved).start())
 

time: 90.8 us -> 90.8 us (level)
  no operation moved by 1% of the time
where the time goes in v8:
time: 90.8 us; the launch traced here: 90.7 us
  Pallas kernels  90.7 us (100%)
    pallas_call x1, Pallas kernels, layer(): pl.pallas_call(layer_kernel, out_shape=(pltpu.VMEM((chunk, width), F32),...  88.7 us
    pallas_call x1, Pallas kernels, layer(): pl.pallas_call(functools.partial(last_kernel, last_head), out_shape=jax.S...  2 us

profile of v8, /device:TPU:0, one launch (start us, length us, event | category | flops | bytes accessed | tf_op | source)
XLA Modules:
  0.0 90.7 jit_solution(14509694414750261796)
XLA Ops:
  0.0 88.7 %shard_map.64 = (f32[512,3072]{1,0:T(8,128)S(1)}, f32[512,3072]{1,0:T(8,128)S(1)}, bf16[12,512,128]{2,1,0:T(8,128)(2,1)S(1)}, bf16[1536,3072]{1,0:T(8,128)(2,1)S(1)}) custom-call(s32[1,512]{1,0:T(1,128)} %bitcast.1, bf16[512,3072]{1,0:T(8,128)(2,1)} %x_hbm.1, bf16[3072,1536]{1,0:T(8,128)(2,1)} %wq_hbm.1, bf16[3072,512]{1,0:T(8,128)(2,1)} %wk_hbm.1, ...), custom_call_target="tpu_custom_call" | custom-call | tf_op jit(solution)/shard_map/pallas_call | solution.py:376
  88.7 2.0 %shard_map.65 = bf16[512,3072]{1,0:T(8,128)(2,1)} custom-call(f32[512,3072]{1,0:T(8,128)S(1)} %get-tuple-element.9.y_own, f32[512,3072]{1,0:T(8,128)S(1)} %get-tuple-element.10.y_oth, bf16[12,512,128]{2,1,0:T(8,128)(2,1)S(1)} %get-tuple-element.11.o_oth, bf16[1536,3072]{1,0:T(8,128)(2,1)S(1)} %get-tuple-element.12.w_oth), custom_call_target="tpu_custom_call" | custom-call | tf_op jit(solution)/shard_map/pallas_call | solution.py:408
